TPU v7x, 32 devices: a whole 2x2x4 slice. The times are simulated.
32 devices in a mesh: dp: 8 (over z, y), mp: 4 (over x, core).
Axes of the slice: x: 2, y: 2, z: 4, core: 2. Of those that a mesh axis runs over, the one named last changes fastest.
Arguments:
- streams: bfloat16 [2048, 4, 8192], P('dp', None, 'mp'), may hold values from -200 to 200
- branch_out: bfloat16 [2048, 8192], P('dp', 'mp'), may hold values from -6 to 6
- merge_weight: float32 [20, 4, 8192], P(None, None, ('mp', 'dp')), may hold values from -0.03125 to 0.03125
- next_weight: float32 [24, 4, 8192], P(None, None, ('mp', 'dp')), may hold values from -0.03125 to 0.03125
- blend_bias: float32 [44], replicated, may hold values from -3 to 3
- blend_scale: float32 [5], replicated, may hold values from 0.5 to 3
- norm_gain: float32 [8192], P('mp'), may hold values from 0.5 to 1.5
Outputs:
- streams_out: bfloat16 [2048, 4, 8192], P('dp', None, 'mp')
- branch_in: bfloat16 [2048, 8192], P('dp', 'mp')
- next_mix: float32 [2048, 20], P('dp')
All inputs are finite; a program needn't handle non-finite values.
Results may differ from a plain program's by a relative error of at most 0.001.
Values sent between devices are 32-bit elements; how exact they have to be, the bound alone decides.
No kernel may reach another device: no remote copies, remote signals or barrier semaphores. Data moves between devices by JAX's collectives and lax.ppermute only.
A program may use at most 64 MiB of HBM per device.

v0:
```python
import jax
import jax.numpy as jnp
from jax import lax
from jax.sharding import PartitionSpec as P

D = 8192
STREAMS = 4
BALANCE_ROUNDS = 6
epsilon = 1e-06


def balance_normalize(balanced_matrix):
    for balance_round in range(BALANCE_ROUNDS):
        balanced_matrix = balanced_matrix / jnp.sum(balanced_matrix, axis=2, keepdims=True)
        balanced_matrix = balanced_matrix / jnp.sum(balanced_matrix, axis=1, keepdims=True)
    return balanced_matrix


def settle(columns, finish):
    summed = lax.psum(columns, "mp")
    result = finish(summed)
    return result


def first_coef(raw_sums, squares, blend_bias, blend_scale):
    rms_root = jnp.sqrt(squares / (STREAMS * D) + epsilon)
    score_logits = raw_sums / rms_root[:, None]
    post_mix = 2.0 * jax.nn.sigmoid(blend_scale[0] * score_logits[:, :4] + blend_bias[:4])
    residual_blend = balance_normalize(
        jnp.exp(
            blend_scale[1] * score_logits[:, 4:20].reshape(-1, 4, 4)
            + blend_bias[4:20].reshape(4, 4)
        )
    )
    return (post_mix, residual_blend)


def second_coef(raw_sums, squares, blend_bias, blend_scale):
    rms_root = jnp.sqrt(squares / (STREAMS * D) + epsilon)
    score_logits = raw_sums / rms_root[:, None]
    pre_next = jax.nn.sigmoid(blend_scale[2] * score_logits[:, :4] + blend_bias[20:24])
    post_next = 2.0 * jax.nn.sigmoid(blend_scale[3] * score_logits[:, 4:8] + blend_bias[24:28])
    residual_following = balance_normalize(
        jnp.exp(
            blend_scale[4] * score_logits[:, 8:24].reshape(-1, 4, 4)
            + blend_bias[28:44].reshape(4, 4)
        )
    )
    return (pre_next, post_next, residual_following)


def mix_streams(residual_blend, post_mix, streams, branch_out):
    branch_wide = branch_out.astype(jnp.float32)
    outputs = []
    for target in range(STREAMS):
        total = post_mix[:, target, None] * branch_wide
        for source in range(STREAMS):
            total = total + residual_blend[:, target, source, None] * streams[:, source, :].astype(
                jnp.float32
            )
        outputs.append(total)
    return jnp.stack(outputs, axis=1)


def unite(pre_next, mixed):
    total = pre_next[:, 0, None] * mixed[:, 0, :]
    for source in range(1, STREAMS):
        total = total + pre_next[:, source, None] * mixed[:, source, :]
    return total


def local(streams, branch_out, merge_weight, next_weight, blend_bias, blend_scale, norm_gain):
    merge_rows, next_rows = (
        lax.all_gather(merge_weight, "dp", axis=2, tiled=True),
        lax.all_gather(next_weight, "dp", axis=2, tiled=True),
    )
    highest = lax.Precision.HIGHEST
    raw_part = jnp.einsum(
        "tic,kic->tk", streams, merge_rows, precision=highest, preferred_element_type=jnp.float32
    )
    gram_part = jnp.einsum("tic,tjc->tij", streams, streams, preferred_element_type=jnp.float32)
    columns = jnp.concatenate([raw_part, jnp.trace(gram_part, axis1=1, axis2=2)[:, None]], axis=1)

    def finish_first(summed):
        post_mix, residual_blend = first_coef(
            summed[:, :20], summed[:, 20], blend_bias, blend_scale
        )
        return jnp.concatenate([post_mix, residual_blend.reshape(-1, 16)], axis=1)

    merge_coef = settle(columns, finish_first)
    post_mix = merge_coef[:, :4]
    residual_blend = merge_coef[:, 4:20].reshape(-1, 4, 4)
    mixed = mix_streams(residual_blend, post_mix, streams, branch_out)
    streams_out = mixed.astype(jnp.bfloat16)
    raw_next = jnp.einsum("tic,kic->tk", mixed, next_rows, precision=highest)
    extra_cols = jnp.sum(mixed * mixed, axis=(1, 2))[:, None]
    columns_next = jnp.concatenate([raw_next, extra_cols], axis=1)

    def finish_second(summed):
        squares = summed[:, 24]
        pre_next, post_next, residual_following = second_coef(
            summed[:, :24], squares, blend_bias, blend_scale
        )
        pieces = [pre_next, post_next, residual_following.reshape(-1, 16)]
        return jnp.concatenate(pieces, axis=1)

    next_coef = settle(columns_next, finish_second)
    pre_next = next_coef[:, :4]
    next_mix = next_coef[:, 4:24]
    united = unite(pre_next, mixed)
    united_sq = lax.psum(jnp.sum(united * united, axis=1), "mp")
    branch_in = (united / jnp.sqrt(united_sq / D + epsilon)[:, None] * norm_gain).astype(
        jnp.bfloat16
    )
    return (streams_out, branch_in, next_mix)


def solution(mesh):
    placed = (
        P("dp", None, "mp"),
        P("dp", "mp"),
        P(None, None, ("mp", "dp")),
        P(None, None, ("mp", "dp")),
        P(),
        P(),
        P("mp"),
    )
    return jax.shard_map(
        local,
        mesh=mesh,
        in_specs=placed,
        out_specs=(P("dp", None, "mp"), P("dp", "mp"), P("dp", None)),
        check_vma=False,
    )
```

profile of v0, /device:TPU:0, one launch (start us, length us, event | category | flops | bytes accessed | tf_op | source)
XLA Modules:
  0.0 152.0 jit_solution(15976659351027897930)
XLA Ops:
  0.6 0.0 copy-start.7
  0.7 0.0 copy-start.8
  0.7 0.0 copy-start.6
  0.7 0.0 copy-start.5
  0.7 9.4 %fusion.28 = f32[256]{0:T(256)S(1)} fusion(bf16[256,4,2048]{2,1,0:T(4,128)(2,1)} %param.7, pred[4,4]{1,0:T(4,128)(4,1)S(1)} %iota_compare_fusion), kind=kOutput, calls=%fused_computation.54 | convolution fusion | flops 16785152 | bytes 4195344 | tf_op jit(solution)/shard_map/tic,tjc->tij/dot_general | solution.py:81
  10.1 0.0 copy-done.7
  10.1 0.1 fusion.80
  10.2 0.1 add.136
  10.2 0.1 fusion.79
  10.3 0.1 add.168
  10.4 0.0 copy-done.8
  10.4 0.6 fusion.78
  11.0 0.0 copy-done.6
  11.0 0.0 copy-done.5
  11.1 33.9 %all_gather.7 = f32[24,4,2048]{2,0,1:T(8,128)S(1)} all-gather(f32[24,4,256]{2,0,1:T(8,128)S(1)} %copy.16), channel_id=1, replica_groups=mesh['dp'=8,'mp'=4] {'dp'}, dimensions={2}, use_global_device_ids=true | all-gather | bytes 884736 | tf_op jit(solution)/shard_map/all_gather | solution.py:75
  45.0 32.1 %all_gather.6 = f32[20,4,2048]{2,0,1:T(8,128)S(1)} all-gather(f32[20,4,256]{2,0,1:T(8,128)S(1)} %copy.10), channel_id=1, replica_groups=mesh['dp'=8,'mp'=4] {'dp'}, dimensions={2}, use_global_device_ids=true | all-gather | bytes 737280 | tf_op jit(solution)/shard_map/all_gather | solution.py:74
  77.1 9.2 %convolution_bitcast_fusion = f32[256,20]{0,1:T(8,128)S(1)} fusion(f32[20,4,2048]{2,0,1:T(8,128)S(1)} %all_gather.6, bf16[256,4,2048]{2,1,0:T(4,128)(2,1)} %param.7), kind=kOutput, calls=%fused_computation.56 | convolution fusion | flops 503316480 | bytes 4870144 | tf_op jit(solution)/shard_map/tic,kic->tk/dot_general | solution.py:78
  86.3 10.4 %psum.21 = f32[256,21]{0,1:T(8,128)S(1)} all-reduce(f32[256,21]{0,1:T(8,128)S(1)} %pad_maximum_fusion.5), channel_id=1, replica_groups=mesh['dp'=8,'mp'=4] {'mp'}, use_global_device_ids=true, to_apply=%region_1.2 | all-reduce | flops 5376 | bytes 43008 | tf_op jit(solution)/shard_map/psum | solution.py:20
  96.7 0.8 fusion.56
  97.5 0.7 slice_multiply_fusion.1
  98.2 0.1 fusion.74
  98.6 0.0 copy-start.4
  98.6 4.6 %copy.11 = bf16[256,4,2048]{2,0,1:T(8,128)(2,1)S(1)} copy(bf16[256,4,2048]{2,1,0:T(4,128)(2,1)} %param.7) | data formatting | bytes 8388608 | tf_op args[0]
  103.2 0.0 copy-done.4
  103.2 2.3 %fusion.13 = (f32[256,2048]{1,0:T(8,128)S(1)}, f32[256,2048]{1,0:T(8,128)S(1)}) fusion(bf16[256,2048]{1,0:T(8,128)(2,1)S(1)} %copy-done.4, f32[256]{0:T(256)S(1)} %bitcast.135, f32[256]{0:T(256)S(1)} %bitcast.136, f32[256]{0:T(256)S(1)} %bitcast.137, f32[256]{0:T(256)S(1)} %bitcast.130, f32[256]{0:T(256)S(1)} %bitcast.140, ...), kind=kLoop, calls=%fused_computation.35 | loop fusion | flops 12058624 | bytes 9447424 | tf_op jit(solution)/shard_map/add | solution.py:58
  105.5 0.0 copy-start
  105.5 2.3 %fusion.21 = (f32[256,2048]{1,0:T(8,128)S(1)}, f32[256,2048]{1,0:T(8,128)S(1)}) fusion(bf16[256,2048]{1,0:T(8,128)(2,1)S(1)} %copy-done.4, f32[256]{0:T(256)S(1)} %bitcast.126, f32[256]{0:T(256)S(1)} %bitcast.127, f32[256]{0:T(256)S(1)} %bitcast.128, f32[256]{0:T(256)S(1)} %bitcast.129, f32[256]{0:T(256)S(1)} %bitcast.139, ...), kind=kLoop, calls=%fused_computation.43 | loop fusion | flops 12058624 | bytes 9447424 | tf_op jit(solution)/shard_map/add | solution.py:58
  107.8 0.0 copy-start.2
  107.8 0.0 copy-start.3
  107.8 6.6 %fusion.29 = f32[256,24]{0,1:T(8,128)S(1)} fusion(f32[24,4,2048]{2,0,1:T(8,128)S(1)} %all_gather.7, f32[256,1,2048]{2,0,1:T(8,128)S(1)} %bitcast.111, f32[256,1,2048]{2,0,1:T(8,128)S(1)} %bitcast.108, f32[256,1,2048]{2,0,1:T(8,128)S(1)} %bitcast.105, f32[256,1,2048]{2,0,1:T(8,128)S(1)} %bitcast.102), kind=kOutput, calls=%fused_computation.55 | convolution fusion | flops 610271232 | bytes 9199616 | tf_op jit(solution)/shard_map/tic,kic->tk/dot_general | solution.py:95
  114.4 0.0 copy-done
  114.4 0.0 copy-done.2
  114.4 0.0 copy-done.3
  114.4 0.9 multiply_reduce_fusion
  115.3 10.8 %psum.22 = f32[256,25]{0,1:T(8,128)S(1)} all-reduce(f32[256,25]{0,1:T(8,128)S(1)} %pad_maximum_fusion.4), channel_id=1, replica_groups=mesh['dp'=8,'mp'=4] {'mp'}, use_global_device_ids=true, to_apply=%region_15.16 | all-reduce | flops 6400 | bytes 51200 | tf_op jit(solution)/shard_map/psum | solution.py:20
  126.1 1.4 fusion.45
  127.5 0.6 slice_multiply_fusion
  128.1 0.1 fusion.72
  128.2 0.1 divide_reduce_fusion
  128.3 0.1 divide_reduce_fusion.6
  128.4 0.1 divide_reduce_fusion.5
  128.5 0.1 divide_reduce_fusion.4
  128.7 0.1 divide_reduce_fusion.3
  128.8 0.1 divide_reduce_fusion.2
  128.9 0.7 exponential_divide_fusion
  129.6 0.6 pad_maximum_fusion.6
  130.2 0.0 copy-start.9
  130.2 4.9 %multiply_reduce_fusion.1 = (f32[256]{0:T(256)S(1)}, f32[256,2048]{1,0:T(8,128)}) fusion(f32[256,2048]{1,0:T(8,128)} %copy-done.3, f32[256]{0:T(256)S(1)} %bitcast.143, f32[256,2048]{1,0:T(8,128)} %copy-done.2, f32[256]{0:T(256)S(1)} %bitcast.144, f32[256,2048]{1,0:T(8,128)} %copy-done, f32[256]{0:T(256)S(1)} %bitcast.145, ...), kind=kLoop, calls=%fused_computation.49 | loop fusion | flops 4718336 | bytes 10490880 | tf_op jit(solution)/shard_map/reduce_sum | solution.py:111
  135.1 5.9 %psum.23 = f32[256]{0:T(256)S(1)} all-reduce(f32[256]{0:T(256)S(1)} %get-tuple-element.6), channel_id=1, replica_groups=mesh['dp'=8,'mp'=4] {'mp'}, use_global_device_ids=true, to_apply=%region_17.18 | all-reduce | flops 256 | bytes 2048 | tf_op jit(solution)/shard_map/psum | solution.py:111
  141.0 0.0 copy-start.1
  141.0 0.0 copy-done.9
  141.1 3.0 %multiply_convert_fusion = bf16[256,2048]{1,0:T(8,128)(2,1)} fusion(f32[256,2048]{1,0:T(8,128)} %get-tuple-element.7, f32[2048]{0:T(1024)S(1)} %copy-done.9, f32[256]{0:T(256)S(1)} %add_sqrt_fusion), kind=kLoop, calls=%fused_computation.48 | loop fusion | flops 1572864 | bytes 3154944 | tf_op jit(solution)/shard_map/convert_element_type | solution.py:112
  144.1 0.0 copy-done.1
  144.1 2.6 %fusion.27 = bf16[256,4,2048]{2,0,1:T(8,128)(2,1)S(1)} fusion(f32[256,1,2048]{2,0,1:T(8,128)} %bitcast.113, f32[256,1,2048]{2,0,1:T(8,128)} %bitcast.110, f32[256,1,2048]{2,0,1:T(8,128)S(1)} %bitcast.107, f32[256,1,2048]{2,0,1:T(8,128)S(1)} %bitcast.104), kind=kLoop, calls=%fused_computation.52 | loop fusion | flops 6291456 | bytes 12582912 | tf_op jit(solution)/shard_map/convert_element_type | solution.py:94
  146.7 5.3 %copy.17 = bf16[256,4,2048]{2,1,0:T(4,128)(2,1)} copy(bf16[256,4,2048]{2,0,1:T(8,128)(2,1)S(1)} %fusion.27) | data formatting | bytes 8388608
  (26 shorter events, 0.4 us)
Async XLA Ops:
  0.6 9.4 %copy-start.7 = (f32[44]{0:T(128)S(1)}, f32[44]{0:T(128)}, u32[]{:S(2)}) copy-start(f32[44]{0:T(128)} %param.11) | copy-start | bytes 532
  0.7 9.8 %copy-start.8 = (f32[5]{0:T(128)S(1)}, f32[5]{0:T(128)}, u32[]{:S(2)}) copy-start(f32[5]{0:T(128)} %param.12) | copy-start | bytes 64
  0.7 10.4 %copy-start.6 = (f32[20,4,256]{2,1,0:T(4,128)S(1)}, f32[20,4,256]{2,1,0:T(4,128)}, u32[]{:S(2)}) copy-start(f32[20,4,256]{2,1,0:T(4,128)} %param.9) | copy-start | bytes 245764
  0.7 10.4 %copy-start.5 = (f32[24,4,256]{2,1,0:T(4,128)S(1)}, f32[24,4,256]{2,1,0:T(4,128)}, u32[]{:S(2)}) copy-start(f32[24,4,256]{2,1,0:T(4,128)} %param.10) | copy-start | bytes 294916
  98.6 4.6 %copy-start.4 = (bf16[256,2048]{1,0:T(8,128)(2,1)S(1)}, bf16[256,2048]{1,0:T(8,128)(2,1)}, u32[]{:S(2)}) copy-start(bf16[256,2048]{1,0:T(8,128)(2,1)} %param.8) | copy-start | bytes 3145732
  105.5 8.9 %copy-start = (f32[256,2048]{1,0:T(8,128)}, f32[256,2048]{1,0:T(8,128)S(1)}, u32[]{:S(2)}) copy-start(f32[256,2048]{1,0:T(8,128)S(1)} %get-tuple-element.11) | copy-start | bytes 6291460
  107.8 6.6 %copy-start.2 = (f32[256,2048]{1,0:T(8,128)}, f32[256,2048]{1,0:T(8,128)S(1)}, u32[]{:S(2)}) copy-start(f32[256,2048]{1,0:T(8,128)S(1)} %get-tuple-element.12) | copy-start | bytes 6291460
  107.8 6.6 %copy-start.3 = (f32[256,2048]{1,0:T(8,128)}, f32[256,2048]{1,0:T(8,128)S(1)}, u32[]{:S(2)}) copy-start(f32[256,2048]{1,0:T(8,128)S(1)} %get-tuple-element.13) | copy-start | bytes 6291460
  130.2 10.8 %copy-start.9 = (f32[2048]{0:T(1024)S(1)}, f32[2048]{0:T(1024)}, u32[]{:S(2)}) copy-start(f32[2048]{0:T(1024)} %param.13) | copy-start | bytes 24580
  141.0 3.1 %copy-start.1 = (f32[256,2048]{1,0:T(8,128)S(1)}, f32[256,2048]{1,0:T(8,128)}, u32[]{:S(2)}) copy-start(f32[256,2048]{1,0:T(8,128)} %copy-done) | copy-start | bytes 6291460
where the time goes:
time: 152 us
  blocking collectives  93.1 us (61%)
  matrix products  25.2 us (17%)
  other arithmetic  21.8 us (14%)
  local copies, waits for them, and re-layouts  10.9 us (7%)
    all_gather x1, blocking collectives, local(): lax.all_gather(next_weight, 'dp', axis=2, tiled=True)  33.9 us
    all_gather x1, blocking collectives, local(): lax.all_gather(merge_weight, 'dp', axis=2, tiled=True)  32.1 us
    psum x2, blocking collectives, settle(): summed = lax.psum(columns, 'mp')  21.2 us
    unnamed x26, local copies, waits for them, and re-layouts  9.92 us
    dot_general x1, matrix products, local(): jnp.einsum('tic,tjc->tij', streams, streams, preferred_element_type=jnp.f...  9.4 us
    dot_general x1, matrix products, local(): jnp.einsum('tic,kic->tk', streams, merge_rows, precision=highest, preferr...  9.18 us
    dot_general x1, matrix products, local(): raw_next = jnp.einsum('tic,kic->tk', mixed, next_rows, precision=highest)  6.59 us
    psum x1, blocking collectives, local(): united_sq = lax.psum(jnp.sum(united * united, axis=1), 'mp')  5.92 us

commit v1 on v0

--- a/solution.py
+++ b/solution.py
@@ -9,6 +9,14 @@
 epsilon = 1e-06
 
 
+def sum_by_hops(shard, axis):
+    peers, summed = (lax.axis_size(axis), shard)
+    for reach in [1 << k for k in range(peers.bit_length() - 1)]:
+        pairs = [(i, i ^ reach) for i in range(peers)]
+        summed = summed + lax.ppermute(summed, axis, pairs)
+    return summed
+
+
 def balance_normalize(balanced_matrix):
     for balance_round in range(BALANCE_ROUNDS):
         balanced_matrix = balanced_matrix / jnp.sum(balanced_matrix, axis=2, keepdims=True)
@@ -17,7 +25,7 @@
 
 
 def settle(columns, finish):
-    summed = lax.psum(columns, "mp")
+    summed = sum_by_hops(columns, "mp")
     result = finish(summed)
     return result
 

time: 152 us -> 139 us (0.914)
  blocking collectives: 93.1 us -> 74.8 us
  other arithmetic: 21.8 us -> 24.3 us
  starting transfers between devices: 0 us -> 2.23 us
  matrix products: 25.2 us -> 23.1 us
  local copies, waits for them, and re-layouts: 10.9 us -> 12.6 us
    psum x2 -> x0, blocking collectives: 21.2 us -> none  [settle(): summed = lax.psum(columns, 'mp')]
    ppermute x0 -> x4, starting transfers between devices: none -> 2.23 us  [sum_by_hops(): summed = summed + lax.ppermute(summed, axis, pairs)]
    dot_general x1, matrix products: 9.18 us -> 6.99 us  [local(): jnp.einsum('tic,kic->tk', streams, merge_rows, precision=highest, preferr...]
    all_gather x1, blocking collectives: 32.1 us -> 33.9 us  [local(): lax.all_gather(merge_weight, 'dp', axis=2, tiled=True)]
    add x2, other arithmetic: 4.55 us -> 6.26 us  [mix_streams(): total + residual_blend[:, target, source, None] * streams[:, source, :].a...]
    unnamed x26 -> x28, local copies, waits for them, and re-layouts: 9.92 us -> 11.6 us
  transfers between devices with their start and end apart: 0 -> 4, of which waited for: 0 -> 1; matrix products, arithmetic and copies ran while one was open for 0% -> 10% of each run, Pallas kernels for 0% -> 0%
where the time goes in v1:
time: 139 us
  blocking collectives  74.8 us (54%)
  other arithmetic  24.3 us (17%)
  matrix products  23.1 us (17%)
  local copies, waits for them, and re-layouts  12.6 us (9%)
  starting transfers between devices  2.23 us (2%)
    all_gather x1, blocking collectives, local(): lax.all_gather(next_weight, 'dp', axis=2, tiled=True)  34 us
    all_gather x1, blocking collectives, local(): lax.all_gather(merge_weight, 'dp', axis=2, tiled=True)  33.9 us
    unnamed x28, local copies, waits for them, and re-layouts  11.6 us
    dot_general x1, matrix products, local(): jnp.einsum('tic,tjc->tij', streams, streams, preferred_element_type=jnp.f...  9.5 us
    dot_general x1, matrix products, local(): jnp.einsum('tic,kic->tk', streams, merge_rows, precision=highest, preferr...  6.99 us
    psum x1, blocking collectives, local(): united_sq = lax.psum(jnp.sum(united * united, axis=1), 'mp')  6.83 us
    dot_general x1, matrix products, local(): raw_next = jnp.einsum('tic,kic->tk', mixed, next_rows, precision=highest)  6.59 us
    add x2, other arithmetic, mix_streams(): total + residual_blend[:, target, source, None] * streams[:, source, :].a...  6.26 us
  transfers between devices with their start and end apart: 4, of which 1 were waited for; matrix products, arithmetic and copies ran while one was open for 10% of the time, Pallas kernels for 0%

profile of v1, /device:TPU:0, one launch (start us, length us, event | category | flops | bytes accessed | tf_op | source)
XLA Modules:
  0.0 139.1 jit_solution(13697419002741713066)
XLA Ops:
  0.6 0.9 copy.10
  1.6 33.9 %all_gather.6 = f32[20,4,2048]{2,0,1:T(8,128)S(1)} all-gather(f32[20,4,256]{2,0,1:T(8,128)S(1)} %copy.10), channel_id=1, replica_groups=mesh['dp'=8,'mp'=4] {'dp'}, dimensions={2}, use_global_device_ids=true | all-gather | bytes 737280 | tf_op jit(solution)/shard_map/all_gather | solution.py:82
  35.4 0.0 copy-start.4
  35.4 9.5 %fusion.28 = f32[256]{0:T(256)S(1)} fusion(bf16[256,4,2048]{2,1,0:T(4,128)(2,1)} %param.7, pred[4,4]{1,0:T(4,128)(4,1)S(1)} %iota_compare_fusion), kind=kOutput, calls=%fused_computation.54 | convolution fusion | flops 16785152 | bytes 4195344 | tf_op jit(solution)/shard_map/tic,tjc->tij/dot_general | solution.py:89
  44.9 0.0 copy-done.4
  44.9 0.0 copy-start.8
  44.9 0.0 copy-start.7
  45.0 0.0 copy-start.9
  45.0 7.0 %convolution_bitcast_fusion = f32[256,20]{0,1:T(8,128)S(1)} fusion(f32[20,4,2048]{2,0,1:T(8,128)S(1)} %all_gather.6, bf16[256,4,2048]{2,1,0:T(4,128)(2,1)S(1)} %copy-done.4), kind=kOutput, calls=%fused_computation.56 | convolution fusion | flops 503316480 | bytes 4870144 | tf_op jit(solution)/shard_map/tic,kic->tk/dot_general | solution.py:86
  52.0 0.1 collective-permute-start
  52.1 0.0 copy-done.8
  52.1 0.1 fusion.80
  52.1 0.0 copy-done.7
  52.2 34.0 %all_gather.7 = f32[24,4,2048]{2,0,1:T(8,128)} all-gather(f32[24,4,256]{2,0,1:T(8,128)S(1)} %copy.16), channel_id=1, replica_groups=mesh['dp'=8,'mp'=4] {'dp'}, dimensions={2}, use_global_device_ids=true | all-gather | bytes 884736 | tf_op jit(solution)/shard_map/all_gather | solution.py:83
  86.2 0.1 fusion.81
  86.3 0.0 collective-permute-done
  86.3 1.6 %collective-permute-start.1 = (f32[256,21]{0,1:T(8,128)S(1)}, f32[256,21]{0,1:T(8,128)S(1)}, u32[]{:S(2)}, u32[]{:S(2)}) collective-permute-start(f32[256,21]{0,1:T(8,128)S(1)} %fusion.86), channel_id=1, source_target_pairs={{0,2},{1,3},{2,0},{3,1},{4,6},{5,7},{6,4},{7,5},{8,10},{9,11},{10,... | collective-permute-start | bytes 64520 | tf_op jit(solution)/shard_map/ppermute | solution.py:16
  87.9 0.0 copy-done.9
  87.9 0.7 fusion.79
  88.5 4.3 %copy.11 = bf16[256,4,2048]{2,0,1:T(8,128)(2,1)} copy(bf16[256,4,2048]{2,1,0:T(4,128)(2,1)S(1)} %copy-done.4) | data formatting | bytes 8388608 | tf_op args[0]
  92.8 0.0 copy-start.5
  92.8 0.1 add.146
  92.9 0.0 collective-permute-done.1
  93.0 0.8 slice_multiply_fusion.1
  93.7 0.6 fusion.56
  94.4 0.1 fusion.75
  94.8 0.0 copy-done.5
  94.8 0.0 copy-start
  94.8 4.0 %fusion.13 = (f32[256,2048]{1,0:T(8,128)S(1)}, f32[256,2048]{1,0:T(8,128)S(1)}) fusion(bf16[256,2048]{1,0:T(8,128)(2,1)S(1)} %copy-done.5, f32[256]{0:T(256)S(1)} %bitcast.138, f32[256]{0:T(256)S(1)} %bitcast.139, f32[256]{0:T(256)S(1)} %bitcast.140, f32[256]{0:T(256)S(1)} %bitcast.133, f32[256]{0:T(256)S(1)} %bitcast.143, bf16[256,4,2048]{2,0,1:T(8,128)(2,1)} %copy.11, ...), kind=kLoop, calls=%fused_computation.35 | loop fusion | flops 12058624 | bytes 9447424 | tf_op jit(solution)/shard_map/add | solution.py:66
  98.8 0.0 copy-start.1
  98.8 0.0 copy-done
  98.8 2.3 %fusion.21 = (f32[256,2048]{1,0:T(8,128)S(1)}, f32[256,2048]{1,0:T(8,128)S(1)}) fusion(bf16[256,2048]{1,0:T(8,128)(2,1)S(1)} %copy-done.5, f32[256]{0:T(256)S(1)} %bitcast.127, f32[256]{0:T(256)S(1)} %bitcast.128, f32[256]{0:T(256)S(1)} %bitcast.129, f32[256]{0:T(256)S(1)} %bitcast.130, f32[256]{0:T(256)S(1)} %bitcast.142, ...), kind=kLoop, calls=%fused_computation.43 | loop fusion | flops 12058624 | bytes 9447424 | tf_op jit(solution)/shard_map/add | solution.py:66
  101.1 0.0 copy-start.2
  101.1 0.0 copy-start.3
  101.1 0.0 copy-start.6
  101.1 0.9 multiply_reduce_fusion
  102.0 0.0 copy-done.1
  102.0 0.4 copy-done.2
  102.4 0.7 copy-done.3
  103.1 0.0 copy-done.6
  103.1 6.6 %fusion.29 = f32[256,24]{0,1:T(8,128)S(1)} fusion(f32[24,4,2048]{2,0,1:T(8,128)S(1)} %copy-done.6, f32[256,1,2048]{2,0,1:T(8,128)S(1)} %bitcast.112, f32[256,1,2048]{2,0,1:T(8,128)S(1)} %bitcast.109, f32[256,1,2048]{2,0,1:T(8,128)S(1)} %bitcast.106, f32[256,1,2048]{2,0,1:T(8,128)S(1)} %bitcast.103), kind=kOutput, calls=%fused_computation.55 | convolution fusion | flops 610271232 | bytes 9199616 | tf_op jit(solution)/shard_map/tic,kic->tk/dot_general | solution.py:103
  109.7 0.1 collective-permute-start.2
  109.8 0.1 add.180
  109.9 1.1 collective-permute-done.2
  111.0 0.5 collective-permute-start.3
  111.5 3.5 %fusion.27 = bf16[256,4,2048]{2,0,1:T(8,128)(2,1)S(1)} fusion(f32[256,1,2048]{2,0,1:T(8,128)} %bitcast.113, f32[256,1,2048]{2,0,1:T(8,128)} %bitcast.110, f32[256,1,2048]{2,0,1:T(8,128)} %bitcast.107, f32[256,1,2048]{2,0,1:T(8,128)S(1)} %bitcast.104), kind=kLoop, calls=%fused_computation.52 | loop fusion | flops 6291456 | bytes 12582912 | tf_op jit(solution)/shard_map/convert_element_type | solution.py:102
  115.0 5.3 %copy.17 = bf16[256,4,2048]{2,1,0:T(4,128)(2,1)} copy(bf16[256,4,2048]{2,0,1:T(8,128)(2,1)S(1)} %fusion.27) | data formatting | bytes 8388608
  120.2 0.0 collective-permute-done.3
  120.3 1.4 fusion.45
  121.7 0.6 slice_multiply_fusion
  122.3 0.1 fusion.73
  122.4 0.1 divide_reduce_fusion
  122.5 0.1 divide_reduce_fusion.6
  122.6 0.1 divide_reduce_fusion.5
  122.7 0.1 divide_reduce_fusion.4
  122.8 0.1 divide_reduce_fusion.3
  123.0 0.1 divide_reduce_fusion.2
  123.1 0.7 exponential_divide_fusion
  123.8 0.0 copy-start.10
  123.8 4.9 %multiply_reduce_fusion.1 = (f32[256]{0:T(256)S(1)}, f32[256,2048]{1,0:T(8,128)}) fusion(f32[256,2048]{1,0:T(8,128)} %copy-done.3, f32[256]{0:T(256)S(1)} %bitcast.146, f32[256,2048]{1,0:T(8,128)} %copy-done.2, f32[256]{0:T(256)S(1)} %bitcast.147, f32[256,2048]{1,0:T(8,128)} %copy-done.1, f32[256]{0:T(256)S(1)} %bitcast.148, ...), kind=kLoop, calls=%fused_computation.49 | loop fusion | flops 4718336 | bytes 10490880 | tf_op jit(solution)/shard_map/reduce_sum | solution.py:119
  128.7 6.8 %psum.7 = f32[256]{0:T(256)S(1)} all-reduce(f32[256]{0:T(256)S(1)} %get-tuple-element.6), channel_id=1, replica_groups=mesh['dp'=8,'mp'=4] {'mp'}, use_global_device_ids=true, to_apply=%region_15.16 | all-reduce | flops 256 | bytes 2048 | tf_op jit(solution)/shard_map/psum | solution.py:119
  135.6 0.6 pad_maximum_fusion.6
  136.2 0.0 copy-done.10
  136.2 2.9 %multiply_convert_fusion = bf16[256,2048]{1,0:T(8,128)(2,1)} fusion(f32[256,2048]{1,0:T(8,128)} %get-tuple-element.7, f32[2048]{0:T(1024)S(1)} %copy-done.10, f32[256]{0:T(256)S(1)} %add_sqrt_fusion), kind=kLoop, calls=%fused_computation.48 | loop fusion | flops 1572864 | bytes 3154944 | tf_op jit(solution)/shard_map/convert_element_type | solution.py:120
  (29 shorter events, 0.4 us)
Async XLA Ops:
  35.4 9.5 %copy-start.4 = (bf16[256,4,2048]{2,1,0:T(4,128)(2,1)S(1)}, bf16[256,4,2048]{2,1,0:T(4,128)(2,1)}, u32[]{:S(2)}) copy-start(bf16[256,4,2048]{2,1,0:T(4,128)(2,1)} %param.7) | copy-start | bytes 12582916
  44.9 7.1 %copy-start.8 = (f32[44]{0:T(128)S(1)}, f32[44]{0:T(128)}, u32[]{:S(2)}) copy-start(f32[44]{0:T(128)} %param.11) | copy-start | bytes 532
  44.9 7.2 %copy-start.7 = (f32[24,4,256]{2,1,0:T(4,128)S(1)}, f32[24,4,256]{2,1,0:T(4,128)}, u32[]{:S(2)}) copy-start(f32[24,4,256]{2,1,0:T(4,128)} %param.10) | copy-start | bytes 294916
  45.0 42.9 %copy-start.9 = (f32[5]{0:T(128)S(1)}, f32[5]{0:T(128)}, u32[]{:S(2)}) copy-start(f32[5]{0:T(128)} %param.12) | copy-start | bytes 64
  52.0 34.3 %collective-permute-start = (f32[256,21]{0,1:T(8,128)S(1)}, f32[256,21]{0,1:T(8,128)S(1)}, u32[]{:S(2)}, u32[]{:S(2)}) collective-permute-start(f32[256,21]{0,1:T(8,128)S(1)} %pad_maximum_fusion.5), channel_id=1, source_target_pairs={{0,1},{1,0},{2,3},{3,2},{4,5},{5,4},{6,7},{7,6},{8,9},{9,8},{10,11... | collective-permute-start | bytes 64520 | tf_op jit(solution)/shard_map/ppermute | solution.py:16
  86.3 6.6 %collective-permute-start.1 = (f32[256,21]{0,1:T(8,128)S(1)}, f32[256,21]{0,1:T(8,128)S(1)}, u32[]{:S(2)}, u32[]{:S(2)}) collective-permute-start(f32[256,21]{0,1:T(8,128)S(1)} %fusion.86), channel_id=1, source_target_pairs={{0,2},{1,3},{2,0},{3,1},{4,6},{5,7},{6,4},{7,5},{8,10},{9,11},{10,... | collective-permute-start | bytes 64520 | tf_op jit(solution)/shard_map/ppermute | solution.py:16
  92.8 1.9 %copy-start.5 = (bf16[256,2048]{1,0:T(8,128)(2,1)S(1)}, bf16[256,2048]{1,0:T(8,128)(2,1)}, u32[]{:S(2)}) copy-start(bf16[256,2048]{1,0:T(8,128)(2,1)} %param.8) | copy-start | bytes 3145732
  94.8 4.0 %copy-start = (bf16[256,4,2048]{2,0,1:T(8,128)(2,1)S(1)}, bf16[256,4,2048]{2,0,1:T(8,128)(2,1)}, u32[]{:S(2)}) copy-start(bf16[256,4,2048]{2,0,1:T(8,128)(2,1)} %copy.11) | copy-start | bytes 12582916
  98.8 3.2 %copy-start.1 = (f32[256,2048]{1,0:T(8,128)}, f32[256,2048]{1,0:T(8,128)S(1)}, u32[]{:S(2)}) copy-start(f32[256,2048]{1,0:T(8,128)S(1)} %get-tuple-element.11) | copy-start | bytes 6291460
  101.1 1.3 copy-start.2
  101.1 2.0 %copy-start.3 = (f32[256,2048]{1,0:T(8,128)}, f32[256,2048]{1,0:T(8,128)S(1)}, u32[]{:S(2)}) copy-start(f32[256,2048]{1,0:T(8,128)S(1)} %get-tuple-element.13) | copy-start | bytes 6291460
  101.1 2.0 %copy-start.6 = (f32[24,4,2048]{2,0,1:T(8,128)S(1)}, f32[24,4,2048]{2,0,1:T(8,128)}, u32[]{:S(2)}) copy-start(f32[24,4,2048]{2,0,1:T(8,128)} %all_gather.7) | copy-start | bytes 2359300
  109.7 1.3 collective-permute-start.2
  111.0 9.3 %collective-permute-start.3 = (f32[256,25]{0,1:T(8,128)S(1)}, f32[256,25]{0,1:T(8,128)S(1)}, u32[]{:S(2)}, u32[]{:S(2)}) collective-permute-start(f32[256,25]{0,1:T(8,128)S(1)} %fusion.62), channel_id=1, source_target_pairs={{0,2},{1,3},{2,0},{3,1},{4,6},{5,7},{6,4},{7,5},{8,10},{9,11},{10,... | collective-permute-start | bytes 76808 | tf_op jit(solution)/shard_map/ppermute | solution.py:16
  123.8 12.4 %copy-start.10 = (f32[2048]{0:T(1024)S(1)}, f32[2048]{0:T(1024)}, u32[]{:S(2)}) copy-start(f32[2048]{0:T(1024)} %param.13) | copy-start | bytes 24580
